TPU v7x, 32 devices: a whole 2x2x4 slice. The times are simulated.
32 devices in a mesh: dp: 8 (over z, y), mp: 4 (over x, core).
Axes of the slice: x: 2, y: 2, z: 4, core: 2. Of those that a mesh axis runs over, the one named last changes fastest.
Arguments:
- picture_skip_activations: bfloat16 [16384, 1152], P('dp'), as said below
- caption_closing_activations: bfloat16 [64, 1152], P('dp'), as said below
- normaliser_multipliers: float32 [3, 1152], replicated, may hold values from 0.1 to 1.9
- widening_matrix: bfloat16 [1152, 4304], P('dp', 'mp'), may hold values from -0.1875 to 0.1875
- contracting_matrix: bfloat16 [4304, 1152], P('mp', 'dp'), as said below
- caption_mapping_matrix: bfloat16 [1152, 1152], replicated, as said below
- sharpness_factor: float32 [1], replicated, may hold values from 8 to 32
- score_offset_term: float32 [1], replicated, may hold values from -8 to -3
Outputs:
- row_loss: float32 [64], P('dp')
- col_loss: float32 [64], P('dp')
Inputs may be any that keep to these rules, and one draw needn't show every extreme that they name: `picture_skip_activations`: entries lie within -8 and 8. `caption_closing_activations`: entries lie within -8 and 8. `contracting_matrix`: entries are at most 4.4 / sqrt(4304) in magnitude. `caption_mapping_matrix`: diagonal entries lie within 1 - 2.1 / sqrt(1152) and 1 + 2.1 / sqrt(1152), the others within -2.1 / sqrt(1152) and 2.1 / sqrt(1152).
All inputs are finite; a program needn't handle non-finite values.
Results may differ from a plain program's by a relative error of at most 0.01.
Values may be sent and summed in bfloat16 or wider, within the bound.
A program may use at most 128 MiB of HBM per device.

v0:
```python
import jax
import jax.numpy as jnp
from jax import lax
from jax.sharding import PartitionSpec as P

PATCHES = 256


def layer_norm(values, norm_gain):
    average = jnp.mean(values, axis=-1, keepdims=True)
    centred = values - average
    spread = jnp.mean(centred * centred, axis=-1, keepdims=True)
    return centred * lax.rsqrt(spread + 1e-06) * norm_gain


def unit_vector(vector):
    length = jnp.sqrt(jnp.sum(vector * vector, axis=-1, keepdims=True))
    return (vector / jnp.maximum(length, 1.0)).astype(jnp.bfloat16)


def pool_images(image_final):
    return jnp.mean(image_final.reshape(-1, PATCHES, image_final.shape[1]), axis=1)


def on_device(
    picture_skip_activations,
    caption_closing_activations,
    normaliser_multipliers,
    widening_matrix,
    contracting_matrix,
    caption_mapping_matrix,
    sharpness_factor,
    score_offset_term,
):
    image_rows = picture_skip_activations.astype(jnp.float32)
    image_normed = layer_norm(image_rows, normaliser_multipliers[0]).astype(jnp.bfloat16)
    inner_weight = lax.all_gather(widening_matrix, "dp", axis=0, tiled=True)
    image_units = jax.nn.gelu(
        jnp.dot(image_normed, inner_weight, preferred_element_type=jnp.float32), approximate=True
    ).astype(jnp.bfloat16)
    partial_out = jnp.dot(
        image_units,
        lax.all_gather(contracting_matrix, "dp", axis=1, tiled=True),
        preferred_element_type=jnp.float32,
    )
    unit_share = lax.psum_scatter(
        partial_out.astype(jnp.bfloat16), "mp", scatter_dimension=0, tiled=True
    ).astype(jnp.float32)
    own_count = unit_share.shape[0]
    own_first = lax.axis_index("mp") * own_count
    own_rows = lax.dynamic_slice_in_dim(image_rows, own_first, own_count, 0)
    image_final = layer_norm(own_rows + unit_share, normaliser_multipliers[1])
    own_emb = unit_vector(pool_images(image_final))
    picture_code_direction = lax.all_gather(own_emb, "mp", axis=0, tiled=True)
    text_normed = layer_norm(
        caption_closing_activations.astype(jnp.float32), normaliser_multipliers[2]
    ).astype(jnp.bfloat16)
    text_vector = jnp.dot(text_normed, caption_mapping_matrix, preferred_element_type=jnp.float32)
    caption_code_direction = unit_vector(text_vector)
    offset = lax.axis_index("dp") * picture_code_direction.shape[0]
    matching_scores = (
        sharpness_factor[0]
        * jnp.einsum(
            "pe,qe->pq",
            picture_code_direction,
            lax.all_gather(caption_code_direction, "dp", axis=0, tiled=True),
            preferred_element_type=jnp.float32,
        )
        + score_offset_term[0]
    )
    row_index = offset + lax.broadcasted_iota(jnp.int32, matching_scores.shape, 0)
    col_index = lax.broadcasted_iota(jnp.int32, matching_scores.shape, 1)
    labels = jnp.where(row_index == col_index, 1.0, -1.0).astype(jnp.float32)
    loss_terms = jax.nn.softplus(-labels * matching_scores)
    row_loss = jnp.sum(loss_terms, axis=1)
    col_loss = lax.psum_scatter(jnp.sum(loss_terms, axis=0), "dp", scatter_dimension=0, tiled=True)
    return (row_loss, col_loss)


def solution(mesh):
    return jax.shard_map(
        on_device,
        mesh=mesh,
        in_specs=(P("dp", None), P("dp", None), P(), P("dp", "mp"), P("mp", "dp"), P(), P(), P()),
        out_specs=(P("dp"), P("dp")),
        check_vma=False,
    )
```

profile of v0, /device:TPU:0, one launch (start us, length us, event | category | flops | bytes accessed | tf_op | source)
XLA Modules:
  0.0 232.3 jit_solution(16782825262965968562)
XLA Ops:
  7.2 0.0 copy-start
  7.2 0.0 all-gather.4.cloned.1.call-start
  7.2 0.7 all-gather.4.cloned.1.call-update
  7.9 0.0 all-gather.6.cloned.1.call-start
  8.0 0.7 all-gather.6.cloned.1.call-update
  8.7 0.0 reduce-scatter.2.cloned.1.call-start
  8.7 0.0 copy-start.1
  8.7 0.9 slice_reduce_fusion
  9.7 3.2 %convert_reduce_fusion = f32[2048]{0:T(1024)S(1)} fusion(bf16[2048,1152]{1,0:T(8,128)(2,1)} %param.8), kind=kLoop, calls=%fused_computation.12 | loop fusion | flops 4716544 | bytes 4726784 | tf_op jit(solution)/shard_map/reduce_sum | solution.py:10
  12.9 1.4 multiply_reduce_fusion
  14.3 53.6 %all-gather.4.cloned.1.call-done = bf16[1152,1076]{1,0:T(8,128)(2,1)} async-done(((bf16[144,1076]{1,0:T(8,128)(2,1)}), bf16[1152,1076]{1,0:T(8,128)(2,1)}) %all-gather.4.cloned.1.call-update) | async-done | bytes 2479120 | tf_op jit(solution)/shard_map/all_gather | solution.py:37
  67.9 55.8 %all-gather.6.cloned.1.call-done = bf16[1076,1152]{0,1:T(8,128)(2,1)} async-done(((bf16[1076,144]{0,1:T(8,128)(2,1)}), bf16[1076,1152]{0,1:T(8,128)(2,1)}) %all-gather.6.cloned.1.call-update) | async-done | bytes 2479120 | tf_op jit(solution)/shard_map/all_gather | solution.py:43
  123.7 20.0 %convolution_convert_fusion = bf16[2048,1152]{1,0:T(8,128)(2,1)} fusion(bf16[1076,1152]{0,1:T(8,128)(2,1)} %all-gather.6.cloned.1.call-done, bf16[1152,1076]{1,0:T(8,128)(2,1)} %all-gather.4.cloned.1.call-done, bf16[2048,1152]{1,0:T(8,128)(2,1)} %param.8, f32[1152]{0:T(1024)S(1)} %get-tuple-element.3, f32[2048]{0:T(1024)S(1)} %add_rsqrt_fusion, ...), kind=kOutput, calls=%fused_computation.11 | convolution fusion | flops 10188398592 | bytes 14416384 | tf_op jit(solution)/shard_map/dot_general | solution.py:41
  143.7 0.0 reduce-scatter.2.cloned.1.call-update
  143.7 0.0 copy-start.4
  143.8 7.9 %convert_element_type.27 = f32[2048,1152]{1,0:T(8,128)} convert(bf16[2048,1152]{1,0:T(8,128)(2,1)} %param.8) | non-fusion elementwise | flops 2359296 | bytes 14155776 | tf_op jit(solution)/shard_map/convert_element_type | solution.py:35
  153.0 0.6 dynamic-slice
  154.3 0.1 convert_reduce_fusion.1
  154.4 0.2 fusion.17
  154.6 0.6 multiply_reduce_fusion.2
  155.2 0.1 divide_convert_fusion
  155.3 30.6 %all_gather.15 = bf16[64,1152]{1,0:T(8,128)(2,1)S(1)} all-gather(bf16[8,1152]{1,0:T(8,128)(2,1)S(1)} %divide_convert_fusion), channel_id=1, replica_groups=mesh['dp'=8,'mp'=4] {'dp'}, dimensions={0}, use_global_device_ids=true | all-gather | bytes 165888 | tf_op jit(solution)/shard_map/all_gather | solution.py:66
  185.9 4.5 %reduce-scatter.2.cloned.1.call-done = bf16[512,1152]{1,0:T(8,128)(2,1)} async-done(((bf16[2048,1152]{1,0:T(8,128)(2,1)}), bf16[512,1152]{1,0:T(8,128)(2,1)}) %reduce-scatter.2.cloned.1.call-update) | async-done | bytes 1179664 | tf_op jit(solution)/shard_map/reduce_scatter | solution.py:46
  190.4 2.4 %fusion.14 = f32[512]{0:T(512)S(1)} fusion(bf16[512,1152]{1,0:T(8,128)(2,1)} %reduce-scatter.2.cloned.1.call-done, f32[2048,1152]{1,0:T(8,128)} %convert_element_type.27, s32[]{:T(128)S(6)} %select_n.12), kind=kLoop, calls=%fused_computation.24 | loop fusion | flops 1768960 | bytes 3540996 | tf_op jit(solution)/shard_map/reduce_sum | solution.py:10
  192.9 2.5 %multiply_reduce_fusion.1 = f32[512]{0:T(512)S(1)} fusion(f32[512]{0:T(512)S(1)} %broadcast_multiply_fusion.1, bf16[512,1152]{1,0:T(8,128)(2,1)} %reduce-scatter.2.cloned.1.call-done, f32[2048,1152]{1,0:T(8,128)} %convert_element_type.27, s32[]{:T(128)S(6)} %select_n.12), kind=kLoop, calls=%fused_computation.19 | loop fusion | flops 2948608 | bytes 3543044 | tf_op jit(solution)/shard_map/reduce_sum | solution.py:12
  195.4 2.2 bitcast_reduce_fusion
  197.6 0.1 multiply_reduce_fusion.3
  197.7 0.1 fusion.25
  197.8 5.2 %all-gather = bf16[4,2,1152]{2,1,0:T(2,128)(2,1)S(1)} all-gather(bf16[1,2,1152]{2,1,0:T(2,128)(2,1)S(1)} %fusion.25), channel_id=1, replica_groups=mesh['dp'=8,'mp'=4] {'mp'}, dimensions={0}, use_global_device_ids=true | all-gather | bytes 23040 | tf_op jit(solution)/shard_map/all_gather | solution.py:54
  203.0 0.8 fusion.30
  203.8 21.3 %all-reduce = f32[64]{0:T(128)S(1)} all-reduce(f32[64]{0:T(128)S(1)} %get-tuple-element.5), channel_id=3, replica_groups=mesh['dp'=8,'mp'=4] {'dp'}, use_global_device_ids=true, to_apply=%region_12.13.clone | all-reduce | flops 64 | bytes 512
  225.2 0.6 dynamic-slice.1
  (17 shorter events, 0.1 us)
Async XLA Ops:
  7.2 147.4 %copy-start = (bf16[1152,1152]{1,0:T(8,128)(2,1)S(1)}, bf16[1152,1152]{1,0:T(8,128)(2,1)}, u32[]{:S(2)}) copy-start(bf16[1152,1152]{1,0:T(8,128)(2,1)} %param.13) | copy-start | bytes 7962628
  7.2 60.7 %all-gather.4.cloned.1.call-start = ((), (), s32[]{:S(2)}) async-start(), calls=%async_computation.1 | async-start | bytes 2985984 | tf_op jit(solution)/shard_map/all_gather | solution.py:37
  7.9 115.7 %all-gather.6.cloned.1.call-start = ((), (), s32[]{:S(2)}) async-start(), calls=%async_computation.2 | async-start | bytes 2985984 | tf_op jit(solution)/shard_map/all_gather | solution.py:43
  8.7 181.8 %reduce-scatter.2.cloned.1.call-start = ((), (), s32[]{:S(2)}) async-start(), calls=%async_computation.3 | async-start | bytes 5898240 | tf_op jit(solution)/shard_map/reduce_scatter | solution.py:46
  8.7 4.2 %copy-start.1 = (bf16[2048,1152]{1,0:T(8,128)(2,1)S(1)}, bf16[2048,1152]{1,0:T(8,128)(2,1)}, u32[]{:S(2)}) copy-start(bf16[2048,1152]{1,0:T(8,128)(2,1)} %param.8) | copy-start | bytes 14155780
  143.7 9.3 %copy-start.4 = (u32[32]{0:T(128)S(1)}, u32[32]{0:T(128)}, u32[]{:S(2)}) copy-start(u32[32]{0:T(128)} %constant.53) | copy-start | bytes 388
  143.7 10.5 %copy-start.3 = (bf16[8,1152]{1,0:T(8,128)(2,1)S(1)}, bf16[8,1152]{1,0:T(8,128)(2,1)}, u32[]{:S(2)}) copy-start(bf16[8,1152]{1,0:T(8,128)(2,1)} %param.9) | copy-start | bytes 55300
  190.4 5.0 %copy-start.2 = (bf16[512,1152]{1,0:T(8,128)(2,1)S(1)}, bf16[512,1152]{1,0:T(8,128)(2,1)}, u32[]{:S(2)}) copy-start(bf16[512,1152]{1,0:T(8,128)(2,1)} %reduce-scatter.2.cloned.1.call-done) | copy-start | bytes 3538948
Sparse Core Ops, SparseCore 0:
  10.2 57.6 all-gather.3
  70.1 53.5 all-gather.5
  143.8 46.5 reduce-scatter.1
where the time goes:
time: 233 us; the launch traced here: 232 us
  waiting for transfers between devices  115 us (49%)
  blocking collectives  57.1 us (25%)
  matrix products  21.5 us (9%)
  other arithmetic  20.3 us (9%)
  between operations  15.8 us (7%)
    all_gather x1, waiting for transfers between devices, on_device(): lax.all_gather(contracting_matrix, 'dp', axis=1, tiled=True)  55.8 us
    all_gather x1, waiting for transfers between devices, on_device(): inner_weight = lax.all_gather(widening_matrix, 'dp', axis=0, tiled=True)  53.6 us
    all_gather x1, blocking collectives, on_device(): lax.all_gather(caption_code_direction, 'dp', axis=0, tiled=True)  30.6 us
    unnamed x1, blocking collectives  21.3 us
    dot_general x1, matrix products, on_device(): jnp.dot(image_units, lax.all_gather(contracting_matrix, 'dp', axis=1, til...  20 us
    convert_element_type x1, other arithmetic, on_device(): image_rows = picture_skip_activations.astype(jnp.float32)  7.92 us
    reduce_sum x3, other arithmetic, layer_norm(): average = jnp.mean(values, axis=-1, keepdims=True)  5.79 us
    all_gather x1, blocking collectives, on_device(): picture_code_direction = lax.all_gather(own_emb, 'mp', axis=0, tiled=True)  5.21 us
  transfers between devices with their start and end apart: 3, of which 3 were waited for; matrix products, arithmetic and copies ran while one was open for 7% of the time, Pallas kernels for 0%

commit v1 on v0

--- a/solution.py
+++ b/solution.py
@@ -4,6 +4,16 @@
 from jax.sharding import PartitionSpec as P
 
 PATCHES = 256
+
+
+def gather_around(x, axis, dim):
+    ways, here, turn = (lax.axis_size(axis), lax.axis_index(axis), x.shape[dim])
+    lengths = [n * ways if d == dim else n for d, n in enumerate(x.shape)]
+    full = lax.dynamic_update_slice_in_dim(jnp.zeros(lengths, x.dtype), x, here * turn, axis=dim)
+    for far in range(1, ways):
+        x = lax.ppermute(x, axis, [(d, (d + 1) % ways) for d in range(ways)])
+        full = lax.dynamic_update_slice_in_dim(full, x, (here - far) % ways * turn, axis=dim)
+    return full
 
 
 def layer_norm(values, norm_gain):
@@ -39,9 +49,7 @@
         jnp.dot(image_normed, inner_weight, preferred_element_type=jnp.float32), approximate=True
     ).astype(jnp.bfloat16)
     partial_out = jnp.dot(
-        image_units,
-        lax.all_gather(contracting_matrix, "dp", axis=1, tiled=True),
-        preferred_element_type=jnp.float32,
+        image_units, gather_around(contracting_matrix, "dp", 1), preferred_element_type=jnp.float32
     )
     unit_share = lax.psum_scatter(
         partial_out.astype(jnp.bfloat16), "mp", scatter_dimension=0, tiled=True

time: 233 us -> 217 us (0.931)
  waiting for transfers between devices: 115 us -> 87.8 us
  local copies, waits for them, and re-layouts: 2.17 us -> 11 us
  starting transfers between devices: 0.11 us -> 3.14 us
    ppermute x0 -> x7, waiting for transfers between devices: none -> 83.6 us  [gather_around(): x = lax.ppermute(x, axis, [(d, (d + 1) % ways) for d in range(ways)])]
    all_gather x1 -> x0, waiting for transfers between devices: 55.8 us -> none  [on_device(): lax.all_gather(contracting_matrix, 'dp', axis=1, tiled=True)]
    all_gather x1, waiting for transfers between devices: 53.6 us -> 0.01 us  [on_device(): inner_weight = lax.all_gather(widening_matrix, 'dp', axis=0, tiled=True)]
    dynamic_update_slice x0 -> x8, local copies, waits for them, and re-layouts: none -> 7.98 us  [the longest x7 7.22 us: gather_around(): lax.dynamic_update_slice_in_dim(full, x, (here - far) % ways * turn, axis...]
    ppermute x0 -> x7, starting transfers between devices: none -> 3.06 us  [gather_around(): x = lax.ppermute(x, axis, [(d, (d + 1) % ways) for d in range(ways)])]
  transfers between devices with their start and end apart: 3 -> 9, of which waited for: 3 -> 8; matrix products, arithmetic and copies ran while one was open for 7% -> 11% of each run, Pallas kernels for 0% -> 0%
where the time goes in v1:
time: 217 us; the launch traced here: 216 us
  waiting for transfers between devices  87.8 us (40%)
  blocking collectives  57.1 us (26%)
  matrix products  21.5 us (10%)
  other arithmetic  19.4 us (9%)
  between operations  16.3 us (8%)
  local copies, waits for them, and re-layouts  11 us (5%)
  starting transfers between devices  3.14 us (1%)
    ppermute x7, waiting for transfers between devices, gather_around(): x = lax.ppermute(x, axis, [(d, (d + 1) % ways) for d in range(ways)])  83.6 us
    all_gather x1, blocking collectives, on_device(): lax.all_gather(caption_code_direction, 'dp', axis=0, tiled=True)  30.6 us
    unnamed x1, blocking collectives  21.3 us
    dot_general x1, matrix products, on_device(): jnp.dot(image_units, gather_around(contracting_matrix, 'dp', 1), preferre...  20.1 us
    convert_element_type x1, other arithmetic, on_device(): image_rows = picture_skip_activations.astype(jnp.float32)  7.47 us
    dynamic_update_slice x7, local copies, waits for them, and re-layouts, gather_around(): lax.dynamic_update_slice_in_dim(full, x, (here - far) % ways * turn, axis...  7.22 us
    reduce_sum x3, other arithmetic, layer_norm(): average = jnp.mean(values, axis=-1, keepdims=True)  5.56 us
    all_gather x1, blocking collectives, on_device(): picture_code_direction = lax.all_gather(own_emb, 'mp', axis=0, tiled=True)  5.21 us
  transfers between devices with their start and end apart: 9, of which 8 were waited for; matrix products, arithmetic and copies ran while one was open for 11% of the time, Pallas kernels for 0%

profile of v1, /device:TPU:0, one launch (start us, length us, event | category | flops | bytes accessed | tf_op | source)
XLA Modules:
  0.0 216.1 jit_solution(6189891619524015564)
XLA Ops:
  7.2 0.7 all-gather.3.cloned.1.call-update
  8.0 3.0 %collective-permute-start = (bf16[1076,144]{0,1:T(8,128)(2,1)}, bf16[1076,144]{0,1:T(8,128)(2,1)S(1)}, u32[]{:S(2)}, u32[]{:S(2)}) collective-permute-start(bf16[1076,144]{0,1:T(8,128)(2,1)} %param.12), channel_id=1, source_target_pairs={{0,4},{4,8},{8,12},{12,16},{16,20},{20,24},{24,28},{28,0},{1,5},{5... | collective-permute-start | bytes 929672 | tf_op jit(solution)/shard_map/ppermute | solution.py:14
  11.0 11.0 %collective-permute-done = bf16[1076,144]{0,1:T(8,128)(2,1)S(1)} collective-permute-done((bf16[1076,144]{0,1:T(8,128)(2,1)}, bf16[1076,144]{0,1:T(8,128)(2,1)S(1)}, u32[]{:S(2)}, u32[]{:S(2)}) %collective-permute-start) | collective-permute-done | bytes 309920 | tf_op jit(solution)/shard_map/ppermute | solution.py:14
  22.1 3.0 %convert_reduce_fusion = f32[2048]{0:T(1024)S(1)} fusion(bf16[2048,1152]{1,0:T(8,128)(2,1)} %param.8), kind=kLoop, calls=%fused_computation.12 | loop fusion | flops 4716544 | bytes 4726784 | tf_op jit(solution)/shard_map/reduce_sum | solution.py:20
  25.1 16.9 %collective-permute-done.1 = bf16[1076,144]{0,1:T(8,128)(2,1)} collective-permute-done((bf16[1076,144]{0,1:T(8,128)(2,1)S(1)}, bf16[1076,144]{0,1:T(8,128)(2,1)}, u32[]{:S(2)}, u32[]{:S(2)}) %collective-permute-start.1) | collective-permute-done | bytes 309920 | tf_op jit(solution)/shard_map/ppermute | solution.py:14
  42.0 1.4 multiply_reduce_fusion
  43.6 10.6 %collective-permute-done.2 = bf16[1076,144]{0,1:T(8,128)(2,1)} collective-permute-done((bf16[1076,144]{0,1:T(8,128)(2,1)}, bf16[1076,144]{0,1:T(8,128)(2,1)}, u32[]{:S(2)}, u32[]{:S(2)}) %collective-permute-start.2) | collective-permute-done | bytes 309920 | tf_op jit(solution)/shard_map/ppermute | solution.py:14
  54.2 1.7 broadcast_in_dim.10
  56.0 0.8 constant_dynamic-update-slice_fusion.7
  56.7 16.5 %collective-permute-done.3 = bf16[1076,144]{0,1:T(8,128)(2,1)S(1)} collective-permute-done((bf16[1076,144]{0,1:T(8,128)(2,1)}, bf16[1076,144]{0,1:T(8,128)(2,1)S(1)}, u32[]{:S(2)}, u32[]{:S(2)}) %collective-permute-start.3) | collective-permute-done | bytes 309920 | tf_op jit(solution)/shard_map/ppermute | solution.py:14
  73.2 0.8 constant_dynamic-update-slice_fusion.6
  74.0 1.7 constant_dynamic-update-slice_fusion.5
  75.7 12.8 %collective-permute-done.4 = bf16[1076,144]{0,1:T(8,128)(2,1)S(1)} collective-permute-done((bf16[1076,144]{0,1:T(8,128)(2,1)S(1)}, bf16[1076,144]{0,1:T(8,128)(2,1)S(1)}, u32[]{:S(2)}, u32[]{:S(2)}) %collective-permute-start.4) | collective-permute-done | bytes 309920 | tf_op jit(solution)/shard_map/ppermute | solution.py:14
  88.5 1.7 constant_dynamic-update-slice_fusion.4
  90.2 0.7 constant_dynamic-update-slice_fusion.3
  91.0 7.5 %collective-permute-done.5 = bf16[1076,144]{0,1:T(8,128)(2,1)S(1)} collective-permute-done((bf16[1076,144]{0,1:T(8,128)(2,1)S(1)}, bf16[1076,144]{0,1:T(8,128)(2,1)S(1)}, u32[]{:S(2)}, u32[]{:S(2)}) %collective-permute-start.5) | collective-permute-done | bytes 309920 | tf_op jit(solution)/shard_map/ppermute | solution.py:14
  98.4 0.8 constant_dynamic-update-slice_fusion.2
  99.2 0.7 constant_dynamic-update-slice_fusion.1
  99.9 8.3 %collective-permute-done.6 = bf16[1076,144]{0,1:T(8,128)(2,1)S(1)} collective-permute-done((bf16[1076,144]{0,1:T(8,128)(2,1)S(1)}, bf16[1076,144]{0,1:T(8,128)(2,1)S(1)}, u32[]{:S(2)}, u32[]{:S(2)}) %collective-permute-start.6) | collective-permute-done | bytes 309920 | tf_op jit(solution)/shard_map/ppermute | solution.py:14
  108.2 0.8 constant_dynamic-update-slice_fusion
  109.0 20.1 %convolution_convert_fusion = bf16[2048,1152]{1,0:T(8,128)(2,1)} fusion(bf16[1076,1152]{0,1:T(8,128)(2,1)} %constant_dynamic-update-slice_fusion, bf16[1152,1076]{1,0:T(8,128)(2,1)} %all-gather.3.cloned.1.call-done, bf16[2048,1152]{1,0:T(8,128)(2,1)} %param.8, f32[1152]{0:T(1024)S(1)} %get-tuple-element.3, f32[2048]{0:T(1024)S(1)} %add_rsqrt_fusion, ...), kind=kOutput, calls=%fused_computation.11 | convolution fusion | flops 10188398592 | bytes 14416384 | tf_op jit(solution)/shard_map/dot_general | solution.py:51
  129.1 7.5 %convert_element_type.27 = f32[2048,1152]{1,0:T(8,128)} convert(bf16[2048,1152]{1,0:T(8,128)(2,1)} %param.8) | non-fusion elementwise | flops 2359296 | bytes 14155776 | tf_op jit(solution)/shard_map/convert_element_type | solution.py:45
  139.5 0.6 multiply_reduce_fusion.2
  140.2 30.6 %all_gather.11 = bf16[64,1152]{1,0:T(8,128)(2,1)S(1)} all-gather(bf16[8,1152]{1,0:T(8,128)(2,1)S(1)} %divide_convert_fusion), channel_id=1, replica_groups=mesh['dp'=8,'mp'=4] {'dp'}, dimensions={0}, use_global_device_ids=true | all-gather | bytes 165888 | tf_op jit(solution)/shard_map/all_gather | solution.py:74
  170.8 3.5 %reduce-scatter.2.cloned.1.call-done = bf16[512,1152]{1,0:T(8,128)(2,1)} async-done(((bf16[2048,1152]{1,0:T(8,128)(2,1)}), bf16[512,1152]{1,0:T(8,128)(2,1)}) %reduce-scatter.2.cloned.1.call-update) | async-done | bytes 1179664 | tf_op jit(solution)/shard_map/reduce_scatter | solution.py:54
  174.2 2.4 %fusion.14 = f32[512]{0:T(512)S(1)} fusion(bf16[512,1152]{1,0:T(8,128)(2,1)} %reduce-scatter.2.cloned.1.call-done, f32[2048,1152]{1,0:T(8,128)} %convert_element_type.27, s32[]{:T(128)S(6)} %select_n.67), kind=kLoop, calls=%fused_computation.24 | loop fusion | flops 1768960 | bytes 3540996 | tf_op jit(solution)/shard_map/reduce_sum | solution.py:20
  176.7 2.2 %multiply_reduce_fusion.1 = f32[512]{0:T(512)S(1)} fusion(f32[512]{0:T(512)S(1)} %broadcast_multiply_fusion.1, bf16[512,1152]{1,0:T(8,128)(2,1)S(1)} %copy-done.2, f32[2048,1152]{1,0:T(8,128)} %convert_element_type.27, s32[]{:T(128)S(6)} %select_n.67), kind=kLoop, calls=%fused_computation.19 | loop fusion | flops 2948608 | bytes 3543044 | tf_op jit(solution)/shard_map/reduce_sum | solution.py:22
  178.9 2.2 %bitcast_reduce_fusion = f32[2,1152]{1,0:T(2,128)S(1)} fusion(f32[1152]{0:T(1024)S(1)} %get-tuple-element.4, f32[512]{0:T(512)S(1)} %add_rsqrt_fusion.1, f32[512]{0:T(512)S(1)} %broadcast_multiply_fusion.1, bf16[512,1152]{1,0:T(8,128)(2,1)S(1)} %copy-done.2, f32[2048,1152]{1,0:T(8,128)} %convert_element_type.27, s32[]{:T(128)S(6)} %select_n.67), kind=kLoop, calls=%fused_computation.17 | loop fusion | flops 3536640 | bytes 3556868 | tf_op jit(solution)/shard_map/reduce_sum | solution.py:32
  181.3 5.2 %all-gather = bf16[4,2,1152]{2,1,0:T(2,128)(2,1)S(1)} all-gather(bf16[1,2,1152]{2,1,0:T(2,128)(2,1)S(1)} %fusion.25), channel_id=1, replica_groups=mesh['dp'=8,'mp'=4] {'mp'}, dimensions={0}, use_global_device_ids=true | all-gather | bytes 23040 | tf_op jit(solution)/shard_map/all_gather | solution.py:62
  186.6 0.8 fusion.30
  187.4 21.3 %all-reduce = f32[64]{0:T(128)S(1)} all-reduce(f32[64]{0:T(128)S(1)} %get-tuple-element.5), channel_id=3, replica_groups=mesh['dp'=8,'mp'=4] {'dp'}, use_global_device_ids=true, to_apply=%region_12.13.clone | all-reduce | flops 64 | bytes 512
  208.7 0.6 dynamic-slice.1
  (41 shorter events, 1.4 us)
Async XLA Ops:
  7.2 132.3 %copy-start = (bf16[1152,1152]{1,0:T(8,128)(2,1)S(1)}, bf16[1152,1152]{1,0:T(8,128)(2,1)}, u32[]{:S(2)}) copy-start(bf16[1152,1152]{1,0:T(8,128)(2,1)} %param.13) | copy-start | bytes 7962628
  7.2 101.8 %all-gather.3.cloned.1.call-start = ((), (), s32[]{:S(2)}) async-start(), calls=%async_computation.1 | async-start | bytes 2985984 | tf_op jit(solution)/shard_map/all_gather | solution.py:47
  7.9 166.3 %reduce-scatter.2.cloned.1.call-start = ((), (), s32[]{:S(2)}) async-start(), calls=%async_computation.2 | async-start | bytes 5898240 | tf_op jit(solution)/shard_map/reduce_scatter | solution.py:54
  8.0 34.1 %copy-start.1 = (bf16[2048,1152]{1,0:T(8,128)(2,1)S(1)}, bf16[2048,1152]{1,0:T(8,128)(2,1)}, u32[]{:S(2)}) copy-start(bf16[2048,1152]{1,0:T(8,128)(2,1)} %param.8) | copy-start | bytes 14155780
  8.0 14.1 %collective-permute-start = (bf16[1076,144]{0,1:T(8,128)(2,1)}, bf16[1076,144]{0,1:T(8,128)(2,1)S(1)}, u32[]{:S(2)}, u32[]{:S(2)}) collective-permute-start(bf16[1076,144]{0,1:T(8,128)(2,1)} %param.12), channel_id=1, source_target_pairs={{0,4},{4,8},{8,12},{12,16},{16,20},{20,24},{24,28},{28,0},{1,5},{5... | collective-permute-start | bytes 929672 | tf_op jit(solution)/shard_map/ppermute | solution.py:14
  22.1 19.9 %collective-permute-start.1 = (bf16[1076,144]{0,1:T(8,128)(2,1)S(1)}, bf16[1076,144]{0,1:T(8,128)(2,1)}, u32[]{:S(2)}, u32[]{:S(2)}) collective-permute-start(bf16[1076,144]{0,1:T(8,128)(2,1)S(1)} %collective-permute-done), channel_id=1, source_target_pairs={{0,4},{4,8},{8,12},{12,16},{16,20},{20,24},{24,28},{28,0},{1,5},{5... | collective-permute-start | bytes 929672 | tf_op jit(solution)/shard_map/ppermute | solution.py:14
  25.1 29.1 %copy-start.5 = (f32[3,1152]{1,0:T(4,128)S(1)}, f32[3,1152]{1,0:T(4,128)}, u32[]{:S(2)}) copy-start(f32[3,1152]{1,0:T(4,128)} %param.10) | copy-start | bytes 41476
  42.0 12.2 %collective-permute-start.2 = (bf16[1076,144]{0,1:T(8,128)(2,1)}, bf16[1076,144]{0,1:T(8,128)(2,1)}, u32[]{:S(2)}, u32[]{:S(2)}) collective-permute-start(bf16[1076,144]{0,1:T(8,128)(2,1)} %collective-permute-done.1), channel_id=1, source_target_pairs={{0,4},{4,8},{8,12},{12,16},{16,20},{20,24},{24,28},{28,0},{1,5},{5... | collective-permute-start | bytes 929672 | tf_op jit(solution)/shard_map/ppermute | solution.py:14
  43.4 12.6 %copy-start.3 = (bf16[1076,144]{0,1:T(8,128)(2,1)S(1)}, bf16[1076,144]{0,1:T(8,128)(2,1)}, u32[]{:S(2)}) copy-start(bf16[1076,144]{0,1:T(8,128)(2,1)} %param.12) | copy-start | bytes 929668
  54.2 19.0 %collective-permute-start.3 = (bf16[1076,144]{0,1:T(8,128)(2,1)}, bf16[1076,144]{0,1:T(8,128)(2,1)S(1)}, u32[]{:S(2)}, u32[]{:S(2)}) collective-permute-start(bf16[1076,144]{0,1:T(8,128)(2,1)} %collective-permute-done.2), channel_id=1, source_target_pairs={{0,4},{4,8},{8,12},{12,16},{16,20},{20,24},{24,28},{28,0},{1,5},{5... | collective-permute-start | bytes 929672 | tf_op jit(solution)/shard_map/ppermute | solution.py:14
  73.2 15.3 %collective-permute-start.4 = (bf16[1076,144]{0,1:T(8,128)(2,1)S(1)}, bf16[1076,144]{0,1:T(8,128)(2,1)S(1)}, u32[]{:S(2)}, u32[]{:S(2)}) collective-permute-start(bf16[1076,144]{0,1:T(8,128)(2,1)S(1)} %collective-permute-done.3), channel_id=1, source_target_pairs={{0,4},{4,8},{8,12},{12,16},{16,20},{20,24},{24,28},{28,0},{1,5},{5... | collective-permute-start | bytes 929672 | tf_op jit(solution)/shard_map/ppermute | solution.py:14
  88.5 9.9 %collective-permute-start.5 = (bf16[1076,144]{0,1:T(8,128)(2,1)S(1)}, bf16[1076,144]{0,1:T(8,128)(2,1)S(1)}, u32[]{:S(2)}, u32[]{:S(2)}) collective-permute-start(bf16[1076,144]{0,1:T(8,128)(2,1)S(1)} %collective-permute-done.4), channel_id=1, source_target_pairs={{0,4},{4,8},{8,12},{12,16},{16,20},{20,24},{24,28},{28,0},{1,5},{5... | collective-permute-start | bytes 929672 | tf_op jit(solution)/shard_map/ppermute | solution.py:14
  98.4 9.8 %collective-permute-start.6 = (bf16[1076,144]{0,1:T(8,128)(2,1)S(1)}, bf16[1076,144]{0,1:T(8,128)(2,1)S(1)}, u32[]{:S(2)}, u32[]{:S(2)}) collective-permute-start(bf16[1076,144]{0,1:T(8,128)(2,1)S(1)} %collective-permute-done.5), channel_id=1, source_target_pairs={{0,4},{4,8},{8,12},{12,16},{16,20},{20,24},{24,28},{28,0},{1,5},{5... | collective-permute-start | bytes 929672 | tf_op jit(solution)/shard_map/ppermute | solution.py:14
  129.1 8.8 %copy-start.6 = (u32[32]{0:T(128)S(1)}, u32[32]{0:T(128)}, u32[]{:S(2)}) copy-start(u32[32]{0:T(128)} %constant.114) | copy-start | bytes 388
  129.1 10.0 %copy-start.4 = (bf16[8,1152]{1,0:T(8,128)(2,1)S(1)}, bf16[8,1152]{1,0:T(8,128)(2,1)}, u32[]{:S(2)}) copy-start(bf16[8,1152]{1,0:T(8,128)(2,1)} %param.9) | copy-start | bytes 55300
  174.2 2.4 %copy-start.2 = (bf16[512,1152]{1,0:T(8,128)(2,1)S(1)}, bf16[512,1152]{1,0:T(8,128)(2,1)}, u32[]{:S(2)}) copy-start(bf16[512,1152]{1,0:T(8,128)(2,1)} %reduce-scatter.2.cloned.1.call-done) | copy-start | bytes 3538948
Sparse Core Ops, SparseCore 0:
  10.2 72.1 all-gather.2
  129.2 44.9 reduce-scatter.1
